TPU v7x, 128 devices: a whole 4x4x4 slice. The times are simulated.
128 devices in a mesh: rows: 128 (over x, z, y, core).
Axes of the slice: x: 4, y: 4, z: 4, core: 2. Of those that a mesh axis runs over, the one named last changes fastest.
Arguments:
- tile_values: float32 [26624, 128, 128], P('rows'), as said below
- tile_row: int32 [26624], P('rows'), may hold values from 0 to 15, as said below
- tile_slot: int32 [26624], P('rows'), may hold values from 0 to 143, as said below
- tile_count: int32 [128], P('rows'), may hold values from 144 to 208, as said below
- requests: int32 [128, 128, 1], P('rows'), may hold values from 0 to 15
- right_side: float32 [2048, 4, 128], P('rows')
Outputs:
- solution: float32 [2048, 4, 128], P('rows')
- hessenberg: float32 [4, 4, 3], replicated
Inputs may be any that keep to these rules, and one draw needn't show every extreme that they name: `tile_row`: tile t < 16 of every device lies in block row t; it is the diagonal tile of that row. `tile_slot`: slot s < 16 is the device's own block s; slot 16 + o + q is the q-th block requested from device o; tile t < 144 of every device uses slot t. `tile_count`: some device uses all 208 slots. requests[d, o, q] is a block index among device o's 16 block rows. `tile_values`: tile t < 16 of every device holds the diagonal block of its row.
All inputs are finite; a program needn't handle non-finite values.
Results may differ from a plain program's by a relative error of at most 0.0003.
Values sent between devices are 32-bit elements; how exact they have to be, the bound alone decides.
A program may use at most 64 MiB of HBM per device.

v0:
```python
import functools

import jax
import jax.numpy as jnp
from jax import lax
from jax.sharding import Mesh
from jax.sharding import PartitionSpec as P

ITERS = 3
ROWS = ("rows_0", "rows_1", "rows_2", "rows_3")


epsilon = 1e-06
highest = lax.Precision.HIGHEST


def by_axis(shard, axes):
    return functools.reduce(lax.psum, axes, shard)


def least_squares(hessenberg, beta_norm):
    krylov = hessenberg.shape[2]
    triangle = hessenberg
    target = jnp.zeros((hessenberg.shape[0], krylov + 1), jnp.float32).at[:, 0].set(beta_norm)
    cosines = []
    sine_list = []
    for column in range(krylov):
        column_vals = triangle[:, :, column]
        for earlier in range(column):
            first_entry = column_vals[:, earlier]
            second = column_vals[:, earlier + 1]
            column_vals = column_vals.at[:, earlier].set(
                cosines[earlier] * first_entry + sine_list[earlier] * second
            )
            column_vals = column_vals.at[:, earlier + 1].set(
                cosines[earlier] * second - sine_list[earlier] * first_entry
            )
        first_entry = column_vals[:, column]
        second = column_vals[:, column + 1]
        radius = jnp.sqrt(first_entry * first_entry + second * second)
        cosine = first_entry / radius
        sine_term = second / radius
        cosines.append(cosine)
        sine_list.append(sine_term)
        column_vals = column_vals.at[:, column].set(radius).at[:, column + 1].set(0.0)
        triangle = triangle.at[:, :, column].set(column_vals)
        leading = target[:, column]
        target = (
            target.at[:, column].set(cosine * leading).at[:, column + 1].set(-sine_term * leading)
        )
    weights = jnp.zeros((hessenberg.shape[0], krylov), jnp.float32)
    for column in reversed(range(krylov)):
        partial_sum = target[:, column] - jnp.sum(
            triangle[:, column, column + 1 : krylov] * weights[:, column + 1 :], axis=1
        )
        weights = weights.at[:, column].set(partial_sum / triangle[:, column, column])
    return weights


def local_squares(vector):
    return jnp.sum(vector * vector, axis=(0, 2))


def on_device(tile_values, tile_row, tile_slot, tile_count, requests, right_side):
    tile_total = tile_values.shape[0]
    row_blocks = right_side.shape[0]
    devices = lax.axis_size(ROWS)
    position = jnp.arange(tile_total, dtype=jnp.int32)
    live_mask = (position < tile_count[0]).astype(jnp.float32)
    block_ids = jnp.arange(row_blocks, dtype=jnp.int32)
    row_onehot = (tile_row[None, :] == block_ids[:, None]).astype(jnp.float32) * live_mask[None, :]
    own_requests = requests[0]
    asked_blocks = lax.all_to_all(
        own_requests, ROWS, split_axis=0, concat_axis=0, tiled=True
    ).reshape(-1)
    beta_norm = jnp.sqrt(by_axis(local_squares(right_side), ROWS) + epsilon)
    basis_list = [right_side / beta_norm[None, :, None]]
    hessenberg = jnp.zeros((right_side.shape[1], ITERS + 1, ITERS), jnp.float32)
    for column in range(ITERS):
        vector = basis_list[column]
        outgoing = vector[asked_blocks].reshape(devices, -1, vector.shape[1], vector.shape[2])
        incoming = lax.all_to_all(outgoing, ROWS, split_axis=0, concat_axis=0, tiled=True)
        slot_table = jnp.concatenate(
            [vector, incoming.reshape(-1, vector.shape[1], vector.shape[2])], axis=0
        )
        picked = slot_table[tile_slot]
        products = jnp.einsum("tij,tkj->tki", tile_values, picked, precision=highest)
        candidate = jnp.einsum("rt,tki->rki", row_onehot, products, precision=highest)
        stacked = jnp.stack(basis_list)
        local_terms = jnp.concatenate(
            [
                jnp.einsum("jrki,rki->jk", stacked, candidate, precision=highest),
                local_squares(candidate)[None, :],
            ],
            axis=0,
        )
        summed = by_axis(local_terms, ROWS)
        coefficients = summed[: column + 1]
        candidate = candidate - jnp.einsum("jk,jrki->rki", coefficients, stacked, precision=highest)
        hessenberg = hessenberg.at[:, : column + 1, column].set(jnp.transpose(coefficients))
        remainder = summed[column + 1] - jnp.sum(coefficients * coefficients, axis=0)
        length = jnp.sqrt(jnp.maximum(remainder, 0.0) + epsilon)
        hessenberg = hessenberg.at[:, column + 1, column].set(length)
        if column + 1 < ITERS:
            basis_list.append(candidate / length[None, :, None])
    weights = least_squares(hessenberg, beta_norm)
    solution = jnp.einsum("kj,jrki->rki", weights, jnp.stack(basis_list), precision=highest)
    return (solution, hessenberg)


def solution(mesh):
    finer = Mesh(mesh.devices.reshape(4, 4, 4, 2), ("rows_0", "rows_1", "rows_2", "rows_3"))
    placed = (
        P(ROWS, None, None),
        P(ROWS),
        P(ROWS),
        P(ROWS),
        P(ROWS, None, None),
        P(ROWS, None, None),
    )
    return jax.shard_map(
        on_device,
        mesh=finer,
        in_specs=placed,
        out_specs=(P(ROWS, None, None), P()),
        check_vma=False,
    )
```

profile of v0, /device:TPU:1, one launch (start us, length us, event | category | flops | bytes accessed | tf_op | source)
XLA Modules:
  0.0 291.7 jit_solution(4035739901747230183)
XLA Ops:
  1.6 9.3 %psum.112 = f32[4]{0:T(128)S(1)} all-reduce(f32[4]{0:T(128)S(1)} %multiply_reduce_fusion.4), channel_id=1, replica_groups=mesh['rows_0'=4,'rows_1'=4,'rows_2'=4,'rows_3'=2] {'rows_0'}, use_global_device_ids=true, to_apply=%region_1.0 | all-reduce | flops 4 | bytes 32 | tf_op jit(solution)/shard_map/psum | solution.py:18
  10.9 9.7 %psum.113 = f32[4]{0:T(128)S(1)} all-reduce(f32[4]{0:T(128)S(1)} %psum.112), channel_id=1, replica_groups=mesh['rows_0'=4,'rows_1'=4,'rows_2'=4,'rows_3'=2] {'rows_1'}, use_global_device_ids=true, to_apply=%region_2.0 | all-reduce | flops 4 | bytes 32 | tf_op jit(solution)/shard_map/psum | solution.py:18
  20.6 8.7 %psum.114 = f32[4]{0:T(128)S(1)} all-reduce(f32[4]{0:T(128)S(1)} %psum.113), channel_id=1, replica_groups=mesh['rows_0'=4,'rows_1'=4,'rows_2'=4,'rows_3'=2] {'rows_2'}, use_global_device_ids=true, to_apply=%region_3.0 | all-reduce | flops 4 | bytes 32 | tf_op jit(solution)/shard_map/psum | solution.py:18
  30.7 10.1 %all-to-all-start = ((s32[128,1,1]{2,1,0:T(1,128)}), s32[128,1,1]{2,1,0:T(1,128)S(1)}, u32[]{:S(2)}, u32[]{:S(2)}) async-start(s32[128,1,1]{2,1,0:T(1,128)} %copy.94), calls=%async_computation | async-start | bytes 131072 | tf_op jit(solution)/shard_map/all_to_all | solution.py:73
  45.1 5.5 %all-to-all-done = s32[128,1,1]{2,1,0:T(1,128)S(1)} async-done(((s32[128,1,1]{2,1,0:T(1,128)}), s32[128,1,1]{2,1,0:T(1,128)S(1)}, u32[]{:S(2)}, u32[]{:S(2)}) %all-to-all-start) | async-done | bytes 544 | tf_op jit(solution)/shard_map/all_to_all | solution.py:73
  54.3 4.9 %all-to-all-start.1 = ((f32[128,1,4,128]{3,2,1,0:T(4,128)}), f32[128,1,4,128]{3,2,1,0:T(4,128)S(1)}, u32[]{:S(2)}, u32[]{:S(2)}) async-start(f32[128,1,4,128]{3,2,1,0:T(4,128)} %bitcast.8), calls=%async_computation.1 | async-start | bytes 524288 | tf_op jit(solution)/shard_map/all_to_all | solution.py:82
  60.6 9.4 %all-to-all-done.1 = f32[128,1,4,128]{3,2,1,0:T(4,128)S(1)} async-done(((f32[128,1,4,128]{3,2,1,0:T(4,128)}), f32[128,1,4,128]{3,2,1,0:T(4,128)S(1)}, u32[]{:S(2)}, u32[]{:S(2)}) %all-to-all-start.1) | async-done | bytes 262176 | tf_op jit(solution)/shard_map/all_to_all | solution.py:82
  70.9 24.2 %fusion.56 = f32[208,4,128]{2,1,0:T(4,128)S(1)} fusion(f32[208,4,128]{2,1,0:T(4,128)S(1)} %gather_fusion.1, f32[208,128,128]{2,1,0:T(8,128)} %param.68), kind=kOutput, calls=%fused_computation.141 | convolution fusion | flops 163577856 | bytes 14483456 | tf_op jit(solution)/shard_map/tij,tkj->tki/dot_general | solution.py:87
  95.8 6.9 %psum.116 = f32[2,4]{1,0:T(2,128)S(1)} all-reduce(f32[2,4]{1,0:T(2,128)S(1)} %pad_maximum_fusion.7), channel_id=1, replica_groups=mesh['rows_0'=4,'rows_1'=4,'rows_2'=4,'rows_3'=2] {'rows_0'}, use_global_device_ids=true, to_apply=%region_6.0 | all-reduce | flops 8 | bytes 64 | tf_op jit(solution)/shard_map/psum | solution.py:18
  102.7 6.9 %psum.117 = f32[2,4]{1,0:T(2,128)S(1)} all-reduce(f32[2,4]{1,0:T(2,128)S(1)} %psum.116), channel_id=1, replica_groups=mesh['rows_0'=4,'rows_1'=4,'rows_2'=4,'rows_3'=2] {'rows_1'}, use_global_device_ids=true, to_apply=%region_7.0 | all-reduce | flops 8 | bytes 64 | tf_op jit(solution)/shard_map/psum | solution.py:18
  109.7 6.9 %psum.118 = f32[2,4]{1,0:T(2,128)S(1)} all-reduce(f32[2,4]{1,0:T(2,128)S(1)} %psum.117), channel_id=1, replica_groups=mesh['rows_0'=4,'rows_1'=4,'rows_2'=4,'rows_3'=2] {'rows_2'}, use_global_device_ids=true, to_apply=%region_8.0 | all-reduce | flops 8 | bytes 64 | tf_op jit(solution)/shard_map/psum | solution.py:18
  116.6 8.6 %psum.119 = f32[2,4]{1,0:T(2,128)S(1)} all-reduce(f32[2,4]{1,0:T(2,128)S(1)} %psum.118), channel_id=1, replica_groups=mesh['rows_0'=4,'rows_1'=4,'rows_2'=4,'rows_3'=2] {'rows_3'}, use_global_device_ids=true, to_apply=%region_9.0 | all-reduce | flops 8 | bytes 64 | tf_op jit(solution)/shard_map/psum | solution.py:18
  134.2 7.5 %all-to-all-done.2 = f32[128,1,4,128]{3,2,1,0:T(4,128)S(1)} async-done(((f32[128,1,4,128]{3,2,1,0:T(4,128)}), f32[128,1,4,128]{3,2,1,0:T(4,128)S(1)}, u32[]{:S(2)}, u32[]{:S(2)}) %all-to-all-start.2) | async-done | bytes 262176 | tf_op jit(solution)/shard_map/all_to_all | solution.py:82
  142.6 24.2 %fusion.57 = f32[208,4,128]{2,1,0:T(4,128)S(1)} fusion(f32[208,4,128]{2,1,0:T(4,128)S(1)} %gather_fusion.3, f32[208,128,128]{2,1,0:T(8,128)} %param.68), kind=kOutput, calls=%fused_computation.142 | convolution fusion | flops 163577856 | bytes 14483456 | tf_op jit(solution)/shard_map/tij,tkj->tki/dot_general | solution.py:87
  168.7 6.8 %psum.120 = f32[3,4]{1,0:T(4,128)S(1)} all-reduce(f32[3,4]{1,0:T(4,128)S(1)} %pad_maximum_fusion.5), channel_id=1, replica_groups=mesh['rows_0'=4,'rows_1'=4,'rows_2'=4,'rows_3'=2] {'rows_0'}, use_global_device_ids=true, to_apply=%region_11.0 | all-reduce | flops 12 | bytes 96 | tf_op jit(solution)/shard_map/psum | solution.py:18
  176.2 6.9 %psum.121 = f32[3,4]{1,0:T(4,128)S(1)} all-reduce(f32[3,4]{1,0:T(4,128)S(1)} %psum.120), channel_id=1, replica_groups=mesh['rows_0'=4,'rows_1'=4,'rows_2'=4,'rows_3'=2] {'rows_1'}, use_global_device_ids=true, to_apply=%region_12.0 | all-reduce | flops 12 | bytes 96 | tf_op jit(solution)/shard_map/psum | solution.py:18
  183.1 6.9 %psum.122 = f32[3,4]{1,0:T(4,128)S(1)} all-reduce(f32[3,4]{1,0:T(4,128)S(1)} %psum.121), channel_id=1, replica_groups=mesh['rows_0'=4,'rows_1'=4,'rows_2'=4,'rows_3'=2] {'rows_2'}, use_global_device_ids=true, to_apply=%region_13.0 | all-reduce | flops 12 | bytes 96 | tf_op jit(solution)/shard_map/psum | solution.py:18
  190.1 8.6 %psum.123 = f32[3,4]{1,0:T(4,128)S(1)} all-reduce(f32[3,4]{1,0:T(4,128)S(1)} %psum.122), channel_id=1, replica_groups=mesh['rows_0'=4,'rows_1'=4,'rows_2'=4,'rows_3'=2] {'rows_3'}, use_global_device_ids=true, to_apply=%region_14.0 | all-reduce | flops 12 | bytes 96 | tf_op jit(solution)/shard_map/psum | solution.py:18
  206.1 9.3 %all-to-all-done.3 = f32[128,1,4,128]{3,2,1,0:T(4,128)S(1)} async-done(((f32[128,1,4,128]{3,2,1,0:T(4,128)}), f32[128,1,4,128]{3,2,1,0:T(4,128)S(1)}, u32[]{:S(2)}, u32[]{:S(2)}) %all-to-all-start.3) | async-done | bytes 262176 | tf_op jit(solution)/shard_map/all_to_all | solution.py:82
  216.3 24.2 %fusion.58 = f32[208,4,128]{2,1,0:T(4,128)S(1)} fusion(f32[208,4,128]{2,1,0:T(4,128)S(1)} %gather_fusion.5, f32[208,128,128]{2,1,0:T(8,128)} %param.68), kind=kOutput, calls=%fused_computation.143 | convolution fusion | flops 163577856 | bytes 14483456 | tf_op jit(solution)/shard_map/tij,tkj->tki/dot_general | solution.py:87
  241.7 6.9 %psum.124 = f32[4,4]{1,0:T(4,128)S(1)} all-reduce(f32[4,4]{1,0:T(4,128)S(1)} %pad_maximum_fusion.6), channel_id=1, replica_groups=mesh['rows_0'=4,'rows_1'=4,'rows_2'=4,'rows_3'=2] {'rows_0'}, use_global_device_ids=true, to_apply=%region_20.0 | all-reduce | flops 16 | bytes 128 | tf_op jit(solution)/shard_map/psum | solution.py:18
  248.6 6.9 %psum.125 = f32[4,4]{1,0:T(4,128)S(1)} all-reduce(f32[4,4]{1,0:T(4,128)S(1)} %psum.124), channel_id=1, replica_groups=mesh['rows_0'=4,'rows_1'=4,'rows_2'=4,'rows_3'=2] {'rows_1'}, use_global_device_ids=true, to_apply=%region_21.0 | all-reduce | flops 16 | bytes 128 | tf_op jit(solution)/shard_map/psum | solution.py:18
  255.6 6.9 %psum.126 = f32[4,4]{1,0:T(4,128)S(1)} all-reduce(f32[4,4]{1,0:T(4,128)S(1)} %psum.125), channel_id=1, replica_groups=mesh['rows_0'=4,'rows_1'=4,'rows_2'=4,'rows_3'=2] {'rows_2'}, use_global_device_ids=true, to_apply=%region_22.0 | all-reduce | flops 16 | bytes 128 | tf_op jit(solution)/shard_map/psum | solution.py:18
  262.4 8.6 %psum.127 = f32[4,4]{1,0:T(4,128)S(1)} all-reduce(f32[4,4]{1,0:T(4,128)S(1)} %psum.126), channel_id=1, replica_groups=mesh['rows_0'=4,'rows_1'=4,'rows_2'=4,'rows_3'=2] {'rows_3'}, use_global_device_ids=true, to_apply=%region_23.0 | all-reduce | flops 16 | bytes 128 | tf_op jit(solution)/shard_map/psum | solution.py:18
  (135 shorter events, 54.8 us)
Async XLA Ops:
  0.6 95.0 %copy-start = (f32[16,4,128]{2,1,0:T(4,128)S(1)}, f32[16,4,128]{2,1,0:T(4,128)}, u32[]{:S(2)}) copy-start(f32[16,4,128]{2,1,0:T(4,128)} %param.73) | copy-start | bytes 98308
  0.6 94.5 %copy-start.1 = (s32[208]{0:T(256)S(1)}, s32[208]{0:T(256)}, u32[]{:S(2)}) copy-start(s32[208]{0:T(256)} %param.69) | copy-start | bytes 2500
  30.7 19.8 %all-to-all-start = ((s32[128,1,1]{2,1,0:T(1,128)}), s32[128,1,1]{2,1,0:T(1,128)S(1)}, u32[]{:S(2)}, u32[]{:S(2)}) async-start(s32[128,1,1]{2,1,0:T(1,128)} %copy.94), calls=%async_computation | async-start | bytes 131072 | tf_op jit(solution)/shard_map/all_to_all | solution.py:73
  54.3 15.6 %all-to-all-start.1 = ((f32[128,1,4,128]{3,2,1,0:T(4,128)}), f32[128,1,4,128]{3,2,1,0:T(4,128)S(1)}, u32[]{:S(2)}, u32[]{:S(2)}) async-start(f32[128,1,4,128]{3,2,1,0:T(4,128)} %bitcast.8), calls=%async_computation.1 | async-start | bytes 524288 | tf_op jit(solution)/shard_map/all_to_all | solution.py:82
  126.7 14.9 %all-to-all-start.2 = ((f32[128,1,4,128]{3,2,1,0:T(4,128)}), f32[128,1,4,128]{3,2,1,0:T(4,128)S(1)}, u32[]{:S(2)}, u32[]{:S(2)}) async-start(f32[128,1,4,128]{3,2,1,0:T(4,128)} %bitcast.16), calls=%async_computation.2 | async-start | bytes 524288 | tf_op jit(solution)/shard_map/all_to_all | solution.py:82
  200.7 14.7 %all-to-all-start.3 = ((f32[128,1,4,128]{3,2,1,0:T(4,128)}), f32[128,1,4,128]{3,2,1,0:T(4,128)S(1)}, u32[]{:S(2)}, u32[]{:S(2)}) async-start(f32[128,1,4,128]{3,2,1,0:T(4,128)} %bitcast.39), calls=%async_computation.3 | async-start | bytes 524288 | tf_op jit(solution)/shard_map/all_to_all | solution.py:82
where the time goes:
time: 296 us; the launch traced here: 292 us
  blocking collectives  119 us (40%)
  matrix products  76 us (26%)
  waiting for transfers between devices  31.6 us (11%)
  other arithmetic  23.8 us (8%)
  starting transfers between devices  22.9 us (8%)
  local copies, waits for them, and re-layouts  16.5 us (6%)
    psum x16, blocking collectives, by_axis(): return functools.reduce(lax.psum, axes, shard)  119 us
    dot_general x3, matrix products, on_device(): jnp.einsum('tij,tkj->tki', tile_values, picked, precision=highest)  72.7 us
    all_to_all x3, waiting for transfers between devices, on_device(): lax.all_to_all(outgoing, ROWS, split_axis=0, concat_axis=0, tiled=True)  26.1 us
    another operation x18, other arithmetic  13.9 us
    all_to_all x3, starting transfers between devices, on_device(): lax.all_to_all(outgoing, ROWS, split_axis=0, concat_axis=0, tiled=True)  12.7 us
    all_to_all x1, starting transfers between devices, on_device(): lax.all_to_all(own_requests, ROWS, split_axis=0, concat_axis=0, tiled=True)  10.1 us
  transfers between devices with their start and end apart: 4, of which 4 were waited for; matrix products, arithmetic and copies ran while one was open for 2% of the time, Pallas kernels for 0%

commit v1 on v0

v1 whole, which is shorter than its diff:
```python
import jax
import jax.numpy as jnp
from jax import lax
from jax.experimental import pallas as pl
from jax.experimental.pallas import tpu as pltpu
from jax.sharding import PartitionSpec as P

MESH = pl.DeviceIdType.MESH
F32 = jnp.float32
BF16 = jnp.bfloat16
EPS = 1e-06
N = 128
RB = 16
TILES = 208
SLOTS = 144
PAIRS = TILES // 2
CHUNK = 16
CHUNKS = TILES // CHUNK
AHEAD = 6


def hops(offset):
    return sum(min(d, 4 - d) for d in ((offset // 2) % 4, (offset // 8) % 4, offset // 32))


OFFSETS = sorted(range(1, N), key=lambda o: (-hops(o), o))


def partner(me, o):
    core = (me % 2 + o % 2) % 2
    y = ((me // 2) % 4 + (o // 2) % 4) % 4
    z = ((me // 8) % 4 + (o // 8) % 4) % 4
    x = (me // 32 + o // 32) % 4
    return ((x * 4 + z) * 4 + y) * 2 + core


def kernel(
    row_s, slot_s, count_s, tiles_hbm, req_ref, b_ref,
    sol_ref, hes_ref,
    raw, wide, left, staged, send, got, ask_out, ask_in, ask_row, ask_s, last_out, last_in,
    load_sem, send_sem, recv_sem, ask_sem,
):
    me = lax.axis_index("rows")
    lane = lax.broadcasted_iota(jnp.int32, (8, 128), 1)
    sub = lax.broadcasted_iota(jnp.int32, (8, 128), 0)
    system = sub % 4
    low = sub < 4

    def load(c):
        part = pl.ds(c * CHUNK, CHUNK)
        return pltpu.make_async_copy(tiles_hbm.at[part], raw.at[part], load_sem.at[c])

    for c in range(CHUNKS):
        load(c).start()
    barrier = pltpu.get_barrier_semaphore()

    def greet(o, carry):
        pl.semaphore_signal(barrier, inc=1, device_id=((me + o) % N,), device_id_type=MESH)
        return carry

    lax.fori_loop(1, N, greet, 0)

    def split(v):
        hi = v.astype(BF16).astype(F32)
        return hi, v - hi

    def prepare(c, carry):
        load(c).wait()
        for i in range(CHUNK):
            t = raw[c * CHUNK + i].T
            hi = t.astype(BF16)
            lo = (t - hi.astype(F32)).astype(BF16)
            side = pl.ds((i % 2) * 128, 128)
            at = c * (CHUNK // 2) + i // 2
            wide[at, pl.ds(0, 128), side] = hi
            wide[at, pl.ds(128, 128), side] = lo
        return carry

    def start_sends(phase, source, target):
        for o in OFFSETS:
            to = partner(me, o)
            pltpu.make_async_remote_copy(
                src_ref=source(to), dst_ref=target.at[me], send_sem=send_sem.at[phase],
                recv_sem=recv_sem.at[phase], device_id=(to,), device_id_type=MESH,
            ).start()

    def wait_all(sem, like):
        whole = like.at[pl.ds(0, N - 1)]
        pltpu.make_async_copy(whole, whole, sem).wait()

    wide_lane = lax.broadcasted_iota(jnp.int32, (N, 1, 128), 2)
    ask_out[...] = jnp.where(wide_lane == me, req_ref[...].reshape(N, 1, 1), 0)

    lax.fori_loop(0, AHEAD, prepare, 0)
    pl.semaphore_wait(barrier, N - 1)
    start_sends(0, lambda to: ask_out.at[to], ask_in)
    ask_in[me] = ask_out[me]
    lax.fori_loop(AHEAD, CHUNKS, prepare, 0)

    def fold(v):
        return v + pltpu.roll(v, 4, 0)

    def product(u, v):
        s = fold(jnp.sum(u * v, axis=0))
        return jnp.broadcast_to(jnp.sum(s, axis=1, keepdims=True), (8, 128))

    def packed(values):
        y = jnp.zeros((8, 128), F32)
        for i, value in enumerate(values):
            y = jnp.where(lane // 16 == i, value, y)
        y = jnp.where((lane % 4 == sub), y, 0.0)
        return jnp.sum(y, axis=0, keepdims=True)

    def unpacked(total, count):
        spread = jnp.broadcast_to(total, (8, 128))
        out = []
        for i in range(count):
            picked = jnp.where(lane == i * 16 + system, spread, 0.0)
            out.append(jnp.broadcast_to(jnp.sum(picked, axis=1, keepdims=True), (8, 128)))
        return out

    def stage(vector, partial):
        for r in range(RB):
            half = (r % 2) * 4
            block = vector[r // 2][half : half + 4]
            staged[r] = jnp.concatenate([block, partial], axis=0)
            hi, lo = split(block)
            left[r] = jnp.concatenate([hi, lo], axis=0)

    def exchange(phase):
        out, into = send.at[phase], got.at[phase]

        def gather(d, carry):
            out[d] = staged[ask_s[0, d]]
            return carry

        lax.fori_loop(0, N, gather, 0, unroll=8)
        start_sends(phase + 1, lambda to: out.at[to], into)
        into[me] = out[me]

    def arrive(phase):
        into = got.at[phase]
        wait_all(recv_sem.at[phase + 1], into)

        def take(c, total):
            for i in range(16):
                d = c * 16 + i
                g = into[d]
                hi, lo = split(g[0:4])
                left[RB + d] = jnp.concatenate([hi, lo], axis=0)
                total = total + g
            return total

        total = lax.fori_loop(0, N // 16, take, jnp.zeros((5, 128), F32))
        return total[4:5]

    def pair(p, slot0, slot1, row0, row1, acc):
        x = jnp.concatenate([left[slot0], left[slot1]], axis=0).astype(BF16)
        x = jnp.concatenate([x, x], axis=1)
        r = jnp.dot(x, wide[p], preferred_element_type=F32)
        for row, value in ((row0, r[0:8, 0:128]), (row1, r[8:16, 128:256])):
            rows = jnp.full((8, 128), row, jnp.int32)
            acc = tuple(acc[q] + jnp.where(rows == q, value, 0.0) for q in range(RB))
        return acc

    def own_tiles():
        acc = []
        for p in range(RB // 2):
            x = jnp.concatenate([left[2 * p], left[2 * p + 1]], axis=0).astype(BF16)
            x = jnp.concatenate([x, x], axis=1)
            r = jnp.dot(x, wide[p], preferred_element_type=F32)
            acc += [r[0:8, 0:128], r[8:16, 128:256]]
        return tuple(acc)

    def other_tiles(acc):
        def known(c, acc):
            for i in range(16):
                p = RB // 2 + c * 16 + i
                acc = pair(p, 2 * p, 2 * p + 1, row_s[2 * p], row_s[2 * p + 1], acc)
            return acc

        def extra(c, acc):
            for i in range(16):
                p = SLOTS // 2 + c * 16 + i
                rows = [jnp.where(t < count_s[0], row_s[t], -1) for t in (2 * p, 2 * p + 1)]
                acc = pair(p, slot_s[2 * p], slot_s[2 * p + 1], rows[0], rows[1], acc)
            return acc

        acc = lax.fori_loop(0, (SLOTS - RB) // 32, known, acc)
        acc = lax.fori_loop(0, (TILES - SLOTS) // 32, extra, acc)
        acc = [fold(a) for a in acc]
        return jnp.stack([jnp.where(low, acc[2 * m], acc[2 * m + 1]) for m in range(RB // 2)])

    def apply(phase):
        exchange(phase)
        acc = own_tiles()
        total = arrive(phase)
        return total, other_tiles(acc)

    b = b_ref[...]
    first_partial = packed([product(b, b)])
    stage(b, first_partial)

    wait_all(recv_sem.at[0], ask_in)
    ask_row[...] = jnp.sum(ask_in[...], axis=0)
    to_scalar = pltpu.make_async_copy(ask_row, ask_s, ask_sem)
    to_scalar.start()
    to_scalar.wait()

    total, z = apply(0)
    (bb,) = unpacked(total, 1)
    beta = jnp.sqrt(bb + EPS)
    inverse = 1.0 / beta
    n00 = bb * inverse * inverse
    v0 = b * inverse
    t1 = z * inverse

    stage(t1, packed([product(t1, v0), product(t1, t1)]))
    total, z = apply(1)
    h00, tt = unpacked(total, 2)
    guess1 = jnp.sqrt(jnp.maximum(tt - 2.0 * h00 * h00 + h00 * h00 * n00, 0.0) + EPS)
    inverse = 1.0 / guess1
    u1 = (t1 - h00 * v0) * inverse
    t2 = (z - h00 * t1) * inverse

    stage(
        t2,
        packed([product(t2, v0), product(t2, u1), product(t2, t2), product(u1, u1), product(u1, v0)]),
    )
    total, z = apply(2)
    q0, q1, qq, m11, m01 = unpacked(total, 5)
    h10 = jnp.sqrt(guess1 * guess1 * m11 + EPS)
    rho = guess1 / h10
    v1 = u1 * rho
    t2 = t2 * rho
    z = z * rho
    d01 = rho * m01
    d11 = rho * rho * m11
    h01 = rho * q0
    x1 = rho * rho * q1
    h11 = x1 - h01 * d01
    square = (
        rho * rho * qq + h01 * h01 * n00 + h11 * h11 * d11
        - 2.0 * (h01 * h01 + h11 * x1) + 2.0 * h01 * h11 * d01
    )
    guess2 = jnp.sqrt(jnp.maximum(square, 0.0) + EPS)
    inverse = 1.0 / guess2
    u2 = (t2 - h01 * v0 - h11 * v1) * inverse
    t3 = (z - h01 * t1 - h11 * t2) * inverse

    last_out[...] = packed(
        [
            product(t3, v0), product(t3, v1), product(t3, u2), product(t3, t3),
            product(u2, u2), product(u2, v0), product(u2, v1),
        ]
    )
    start_sends(4, lambda to: last_out, last_in)
    last_in[me] = last_out[...]
    wait_all(recv_sem.at[4], last_in)
    total = jnp.sum(last_in[...], axis=0)
    p0, p1, p2, pp, m22, m02, m12 = unpacked(total, 7)
    h21 = jnp.sqrt(guess2 * guess2 * m22 + EPS)
    rho = guess2 / h21
    v2 = u2 * rho
    e02 = rho * m02
    e12 = rho * m12
    d22 = rho * rho * m22
    h02 = rho * p0
    x1 = rho * p1
    x2 = rho * rho * p2
    h12 = x1 - h02 * d01
    h22 = x2 - h02 * e02 - h12 * e12
    square = (
        rho * rho * pp + h02 * h02 * n00 + h12 * h12 * d11 + h22 * h22 * d22
        - 2.0 * (h02 * h02 + h12 * x1 + h22 * x2)
        + 2.0 * (h02 * h12 * d01 + h02 * h22 * e02 + h12 * h22 * e12)
    )
    h32 = jnp.sqrt(jnp.maximum(square, 0.0) + EPS)

    def rotation(a, c):
        radius = jnp.sqrt(a * a + c * c)
        return a / radius, c / radius, radius

    c0, s0, r00 = rotation(h00, h10)
    g0, g1 = c0 * beta, -s0 * beta
    r01 = c0 * h01 + s0 * h11
    c1, s1, r11 = rotation(c0 * h11 - s0 * h01, h21)
    g1, g2 = c1 * g1, -s1 * g1
    r02 = c0 * h02 + s0 * h12
    turned = c0 * h12 - s0 * h02
    r12 = c1 * turned + s1 * h22
    c2, s2, r22 = rotation(c1 * h22 - s1 * turned, h32)
    g2 = c2 * g2
    y2 = g2 / r22
    y1 = (g1 - r12 * y2) / r11
    y0 = (g0 - (r01 * y1 + r02 * y2)) / r00
    sol_ref[...] = y0 * v0 + y1 * v1 + y2 * v2

    table = ((h00, h01, h02), (h10, h11, h12), (None, h21, h22), (None, None, h32))
    for k in range(4):
        out = jnp.zeros((4, 3), F32)
        rows = lax.broadcasted_iota(jnp.int32, (4, 3), 0)
        columns = lax.broadcasted_iota(jnp.int32, (4, 3), 1)
        for i in range(4):
            for j in range(3):
                if table[i][j] is not None:
                    value = jnp.broadcast_to(table[i][j][k : k + 1, 0:3], (4, 3))
                    out = jnp.where((rows == i) & (columns == j), value, out)
        hes_ref[k] = out

    wait_all(send_sem.at[0], ask_out)
    for phase in range(3):
        wait_all(send_sem.at[phase + 1], send.at[phase])
    wait_all(send_sem.at[4], last_in)


def solution(mesh):
    def on_device(tile_values, tile_row, tile_slot, tile_count, requests, right_side):
        vmem = pl.BlockSpec(memory_space=pltpu.VMEM)
        smem = pl.BlockSpec(memory_space=pltpu.SMEM)
        answer, hessenberg = pl.pallas_call(
            kernel,
            out_shape=(
                jax.ShapeDtypeStruct((8, 8, 128), F32),
                jax.ShapeDtypeStruct((4, 4, 3), F32),
            ),
            in_specs=[smem, smem, smem, pl.BlockSpec(memory_space=pl.ANY), vmem, vmem],
            out_specs=(vmem, vmem),
            scratch_shapes=[
                pltpu.VMEM((TILES, 128, 128), F32),
                pltpu.VMEM((PAIRS, 256, 256), BF16),
                pltpu.VMEM((SLOTS, 8, 128), F32),
                pltpu.VMEM((RB, 5, 128), F32),
                pltpu.VMEM((3, N, 5, 128), F32),
                pltpu.VMEM((3, N, 5, 128), F32),
                pltpu.VMEM((N, 1, 128), jnp.int32),
                pltpu.VMEM((N, 1, 128), jnp.int32),
                pltpu.VMEM((1, 128), jnp.int32),
                pltpu.SMEM((1, 128), jnp.int32),
                pltpu.VMEM((1, 128), F32),
                pltpu.VMEM((N, 1, 128), F32),
                pltpu.SemaphoreType.DMA((CHUNKS,)),
                pltpu.SemaphoreType.DMA((5,)),
                pltpu.SemaphoreType.DMA((5,)),
                pltpu.SemaphoreType.DMA,
            ],
            compiler_params=pltpu.CompilerParams(
                collective_id=0, has_side_effects=True, vmem_limit_bytes=60 << 20
            ),
            name="arnoldi",
        )(
            tile_row, tile_slot, tile_count, tile_values,
            requests.reshape(N, 1), right_side.reshape(8, 8, 128),
        )
        return answer.reshape(RB, 4, 128), hessenberg

    rows = P("rows")
    return jax.shard_map(
        on_device,
        mesh=mesh,
        in_specs=(rows, rows, rows, rows, rows, rows),
        out_specs=(rows, P()),
        check_vma=False,
    )
```

time: 296 us -> 61.2 us (0.21); the launches traced: 292 us -> 60.9 us
  blocking collectives: 119 us -> 0 us
  matrix products: 76 us -> 0 us
  Pallas kernels: 0 us -> 55.5 us
  waiting for transfers between devices: 31.6 us -> 0 us
  other arithmetic: 23.8 us -> 0 us
  starting transfers between devices: 22.9 us -> 0 us
  local copies, waits for them, and re-layouts: 16.5 us -> 4.14 us
    psum x16 -> x0, blocking collectives: 119 us -> none  [by_axis(): return functools.reduce(lax.psum, axes, shard)]
    dot_general x10 -> x0, matrix products: 76 us -> none  [the longest x3 72.7 us: on_device(): jnp.einsum('tij,tkj->tki', tile_values, picked, precision=highest)]
    pallas_call x0 -> x1, Pallas kernels: none -> 55.5 us  [on_device(): pl.pallas_call(kernel, out_shape=(jax.ShapeDtypeStruct((8, 8, 128), F32),...]
    all_to_all x4 -> x0, waiting for transfers between devices: 31.6 us -> none  [the longest x3 26.1 us: on_device(): lax.all_to_all(outgoing, ROWS, split_axis=0, concat_axis=0, tiled=True)]
    all_to_all x4 -> x0, starting transfers between devices: 22.9 us -> none  [the longest x3 12.7 us: on_device(): lax.all_to_all(outgoing, ROWS, split_axis=0, concat_axis=0, tiled=True)]
    another operation x21 -> x0, other arithmetic: 14 us -> none
    gather x6 -> x0, local copies, waits for them, and re-layouts: 6.99 us -> none  [the longest x3 4.28 us: on_device(): vector[asked_blocks].reshape(devices, -1, vector.shape[1], vector.shape[2])]
    scatter x24 -> x0, local copies, waits for them, and re-layouts: 3.84 us -> none  [the longest x3 2.55 us: on_device(): hessenberg.at[:, :column + 1, column].set(jnp.transpose(coefficients))]
  transfers between devices with their start and end apart: 4 -> 0, of which waited for: 4 -> 0; matrix products, arithmetic and copies ran while one was open for 2% -> 0% of each run, Pallas kernels for 0% -> 0%
where the time goes in v1:
time: 61.2 us; the launch traced here: 60.9 us
  Pallas kernels  55.5 us (91%)
  local copies, waits for them, and re-layouts  4.14 us (7%)
  between operations  1.29 us (2%)
    pallas_call x1, Pallas kernels, on_device(): pl.pallas_call(kernel, out_shape=(jax.ShapeDtypeStruct((8, 8, 128), F32),...  55.5 us
    unnamed x2, local copies, waits for them, and re-layouts  2.76 us
    reshape x1, local copies, waits for them, and re-layouts, on_device(): requests.reshape(N, 1)  1.38 us

profile of v1, /device:TPU:1, one launch (start us, length us, event | category | flops | bytes accessed | tf_op | source)
XLA Modules:
  0.0 60.9 jit_solution(11801734857270426995)
XLA Ops:
  1.3 1.4 %copy.8.req_ref = s32[128,1]{1,0:T(8,128)} copy(s32[128,1]{0,1:T(1,128)} %bitcast.5) | data formatting | bytes 1024 | tf_op jit(solution)/shard_map/reshape | solution.py:353
  2.7 55.5 %arnoldi.1 = (f32[8,8,128]{2,1,0:T(8,128)}, f32[4,4,3]{2,1,0:T(4,128)}) custom-call(s32[208]{0:T(256)} %row_s.1, s32[208]{0:T(256)} %slot_s.1, s32[1]{0:T(128)S(6)} %copy.11.count_s, f32[208,128,128]{2,1,0:T(8,128)} %tiles_hbm.1, s32[128,1]{1,0:T(8,128)} %copy.8.req_ref, f32[8,8,128]{2,1,0:T(8,128)} %bitcast.3), custom_call_target="tpu_custom_call" | custom-call | tf_op jit(solution)/shard_map/arnoldi/pallas_call | solution.py:321
  58.2 1.4 %copy.9 = f32[4,4,3]{1,0,2:T(4,128)} copy(f32[4,4,3]{2,1,0:T(4,128)} %get-tuple-element.7) | data formatting | bytes 384
  59.5 1.4 %copy.12 = f32[16,4,128]{2,1,0:T(4,128)} copy(f32[16,4,128]{2,1,0:T(4,128)} %bitcast.4) | data formatting | bytes 65536

commit v2 on v1

v2 whole, which is shorter than its diff:
```python
import jax
import jax.numpy as jnp
from jax import lax
from jax.experimental import pallas as pl
from jax.experimental.pallas import tpu as pltpu
from jax.sharding import PartitionSpec as P

MESH = pl.DeviceIdType.MESH
F32 = jnp.float32
BF16 = jnp.bfloat16
EPS = 1e-06
N = 128
RB = 16
TILES = 208
SLOTS = 144
PAIRS = TILES // 2
CHUNK = 16
CHUNKS = TILES // CHUNK
AHEAD = 6
FAR = 4
ROWS_AHEAD = 32


def hops(offset):
    return sum(min(d, 4 - d) for d in ((offset // 2) % 4, (offset // 8) % 4, offset // 32))


OFFSETS = sorted(range(1, N), key=lambda o: (-hops(o), o))
CHIPS = sorted(range(0, N, 2), key=lambda o: (hops(o), o))
GROUPS = ([o for o in CHIPS if hops(o) < FAR], [o for o in CHIPS if hops(o) >= FAR])
COUNTS = (2 * len(GROUPS[0]) - 1, 2 * len(GROUPS[1]))


def partners(me):
    def turned(step, size):
        digit = lax.rem(lax.div(me, step), size)
        return [lax.rem(digit + k, size) * step for k in range(size)]

    cores, y, z, x = turned(1, 2), turned(2, 4), turned(8, 4), turned(32, 4)
    return lambda o: cores[o % 2] + (y[o // 2 % 4] + (z[o // 8 % 4] + x[o // 32]))


def kernel(
    count_s, row_hbm, slot_hbm, tiles_hbm, req_hbm, b_hbm,
    sol_ref, hes_ref,
    row_s, slot_s, req_ref, b_ref,
    raw, wide, left, staged, send, got, ask_out, ask_in, ask_row, ask_s, last_out, last_in,
    load_sem, small_sem, send_sem, recv_sem, ask_sem,
):
    me = lax.axis_index("rows")
    partner = partners(me)
    lane = lax.broadcasted_iota(jnp.int32, (8, 128), 1)
    sub = lax.broadcasted_iota(jnp.int32, (8, 128), 0)
    block = lax.broadcasted_iota(jnp.int32, (RB, 8, 128), 0)
    system = sub % 4
    low = sub < 4

    def load(c):
        part = pl.ds(c * CHUNK, CHUNK)
        return pltpu.make_async_copy(tiles_hbm.at[part], raw.at[part], load_sem.at[c])

    small = [
        pltpu.make_async_copy(source, target, small_sem.at[i])
        for i, (source, target) in enumerate(
            ((req_hbm, req_ref), (b_hbm, b_ref), (row_hbm, row_s), (slot_hbm, slot_s))
        )
    ]
    for copy in small:
        copy.start()
    for c in range(CHUNKS):
        load(c).start()
    barrier = pltpu.get_barrier_semaphore()
    for o in OFFSETS:
        pl.semaphore_signal(barrier, inc=1, device_id=(partner(o),), device_id_type=MESH)
    for copy in small:
        copy.wait()

    def split(v):
        hi = v.astype(BF16).astype(F32)
        return hi, v - hi

    def prepare(c, carry):
        load(c).wait()
        for i in range(CHUNK):
            t = raw[c * CHUNK + i].T
            hi = t.astype(BF16)
            lo = (t - hi.astype(F32)).astype(BF16)
            side = pl.ds((i % 2) * 128, 128)
            at = c * (CHUNK // 2) + i // 2
            wide[at, pl.ds(0, 128), side] = hi
            wide[at, pl.ds(128, 128), side] = lo
        return carry

    def start_send(phase, group, to, source, target):
        pltpu.make_async_remote_copy(
            src_ref=source, dst_ref=target.at[me], send_sem=send_sem.at[phase],
            recv_sem=recv_sem.at[phase, group], device_id=(to,), device_id_type=MESH,
        ).start()

    def wait_for(sem, like, count=N - 1):
        whole = like.at[pl.ds(0, count)]
        pltpu.make_async_copy(whole, whole, sem).wait()

    wide_lane = lax.broadcasted_iota(jnp.int32, (N, 128), 1)
    wanted = jnp.broadcast_to(req_ref[...], (N, 128)).T
    ask_out[...] = jnp.where(wide_lane == me, wanted, 0).reshape(N, 1, 128)

    lax.fori_loop(0, AHEAD, prepare, 0)
    pl.semaphore_wait(barrier, N - 1)
    for o in OFFSETS:
        to = partner(o)
        start_send(0, 0, to, ask_out.at[to], ask_in)
    ask_in[me] = ask_out[me]
    lax.fori_loop(AHEAD, CHUNKS, prepare, 0)

    def fold(v):
        return v + pltpu.roll(v, 4, 0)

    def product(u, v):
        s = fold(jnp.sum(u * v, axis=0))
        return jnp.broadcast_to(jnp.sum(s, axis=1, keepdims=True), (8, 128))

    def packed(values):
        y = jnp.zeros((8, 128), F32)
        for i, value in enumerate(values):
            y = jnp.where(lane // 16 == i, value, y)
        y = jnp.where((lane % 4 == sub), y, 0.0)
        return jnp.sum(y, axis=0, keepdims=True)

    def unpacked(total, count):
        spread = jnp.broadcast_to(total, (8, 128))
        out = []
        for i in range(count):
            picked = jnp.where(lane == i * 16 + system, spread, 0.0)
            out.append(jnp.broadcast_to(jnp.sum(picked, axis=1, keepdims=True), (8, 128)))
        return out

    def stage(vector, partial):
        for r in range(RB):
            half = (r % 2) * 4
            block = vector[r // 2][half : half + 4]
            staged[r] = jnp.concatenate([block, partial], axis=0)
            hi, lo = split(block)
            left[r] = jnp.concatenate([hi, lo], axis=0)

    def exchange(phase):
        out, into = send.at[phase], got.at[phase]
        targets = [partner(o) for o in OFFSETS] + [me]

        def fill(i):
            out[targets[i]] = staged[ask_s[0, targets[i]]]

        for i in range(ROWS_AHEAD):
            fill(i)
        for i, o in enumerate(OFFSETS):
            start_send(phase + 1, int(hops(o) >= FAR), targets[i], out.at[targets[i]], into)
            if i + ROWS_AHEAD < N:
                fill(i + ROWS_AHEAD)
        into[me] = staged[ask_s[0, me]]

    def times(p, x0, x1):
        x = jnp.concatenate([x0, x1], axis=0).astype(BF16)
        x = jnp.concatenate([x, x], axis=1)
        r = jnp.dot(x, wide[p], preferred_element_type=F32)
        return r[0:8, 0:128], r[8:16, 128:256]

    def add(acc, row, value):
        return acc + jnp.where(block == row, value, 0.0)

    def own_tiles():
        acc = []
        for p in range(RB // 2):
            acc += times(p, left[2 * p], left[2 * p + 1])
        return jnp.stack(acc)

    def chip_tiles(into, offset, acc):
        first = partner(offset) - lax.rem(me, 2)
        x = []
        for d in (first, first + 1):
            hi, lo = split(into[d][0:4])
            x.append(jnp.concatenate([hi, lo], axis=0))
            left[RB + d] = x[-1]
        y0, y1 = times(RB // 2 + first // 2, x[0], x[1])
        return add(add(acc, row_s[RB + first], y0), row_s[RB + first + 1], y1)

    def extra_tiles(acc):
        for p in range(SLOTS // 2, PAIRS):
            y = times(p, left[slot_s[2 * p]], left[slot_s[2 * p + 1]])
            for t, value in ((2 * p, y[0]), (2 * p + 1, y[1])):
                acc = add(acc, jnp.where(t < count_s[0], row_s[t], -1), value)
        return acc

    def apply(phase, digest):
        exchange(phase)
        into = got.at[phase]
        acc = own_tiles()
        for group in range(2):
            wait_for(recv_sem.at[phase + 1, group], into, COUNTS[group])
            if group == 1:
                total = jnp.sum(into[...], axis=0)
                coefficients = digest(total[4:5])
            for offset in GROUPS[group]:
                acc = chip_tiles(into, offset, acc)
        acc = extra_tiles(acc)
        acc = [fold(acc[r]) for r in range(RB)]
        z = jnp.stack([jnp.where(low, acc[2 * m], acc[2 * m + 1]) for m in range(RB // 2)])
        return coefficients, z

    b = b_ref[...]
    first_partial = packed([product(b, b)])
    stage(b, first_partial)

    wait_for(recv_sem.at[0, 0], ask_in)
    ask_row[...] = jnp.sum(ask_in[...], axis=0)
    to_scalar = pltpu.make_async_copy(ask_row, ask_s, ask_sem)
    to_scalar.start()
    to_scalar.wait()

    def digest0(total):
        (bb,) = unpacked(total, 1)
        beta = jnp.sqrt(bb + EPS)
        inverse = 1.0 / beta
        return beta, inverse, bb * inverse * inverse

    (beta, inverse, n00), z = apply(0, digest0)
    v0 = b * inverse
    t1 = z * inverse
    stage(t1, packed([product(t1, v0), product(t1, t1)]))

    def digest1(total):
        h00, tt = unpacked(total, 2)
        square = tt - 2.0 * h00 * h00 + h00 * h00 * n00
        guess1 = jnp.sqrt(jnp.maximum(square, 0.0) + EPS)
        return h00, guess1, 1.0 / guess1

    (h00, guess1, inverse), z = apply(1, digest1)
    u1 = (t1 - h00 * v0) * inverse
    t2 = (z - h00 * t1) * inverse
    stage(
        t2,
        packed([product(t2, v0), product(t2, u1), product(t2, t2), product(u1, u1), product(u1, v0)]),
    )

    def digest2(total):
        q0, q1, qq, m11, m01 = unpacked(total, 5)
        h10 = jnp.sqrt(guess1 * guess1 * m11 + EPS)
        rho = guess1 / h10
        d01 = rho * m01
        d11 = rho * rho * m11
        h01 = rho * q0
        x1 = rho * rho * q1
        h11 = x1 - h01 * d01
        square = (
            rho * rho * qq + h01 * h01 * n00 + h11 * h11 * d11
            - 2.0 * (h01 * h01 + h11 * x1) + 2.0 * h01 * h11 * d01
        )
        guess2 = jnp.sqrt(jnp.maximum(square, 0.0) + EPS)
        return h10, rho, d01, d11, h01, h11, guess2, 1.0 / guess2

    (h10, rho, d01, d11, h01, h11, guess2, inverse), z = apply(2, digest2)
    v1 = u1 * rho
    t2 = t2 * rho
    u2 = (t2 - h01 * v0 - h11 * v1) * inverse
    t3 = (z * rho - h01 * t1 - h11 * t2) * inverse

    last_out[...] = packed(
        [
            product(t3, v0), product(t3, v1), product(t3, u2), product(t3, t3),
            product(u2, u2), product(u2, v0), product(u2, v1),
        ]
    )
    last_in[me] = last_out[...]
    for o in OFFSETS:
        start_send(4, 0, partner(o), last_out, last_in)

    def rotation(a, c):
        radius = jnp.sqrt(a * a + c * c)
        return a / radius, c / radius, radius

    c0, s0, r00 = rotation(h00, h10)
    g0, g1 = c0 * beta, -s0 * beta
    r01 = c0 * h01 + s0 * h11
    turned1 = c0 * h11 - s0 * h01

    wait_for(recv_sem.at[4, 0], last_in)
    total = jnp.sum(last_in[...], axis=0)
    p0, p1, p2, pp, m22, m02, m12 = unpacked(total, 7)
    h21 = jnp.sqrt(guess2 * guess2 * m22 + EPS)
    rho = guess2 / h21
    v2 = u2 * rho
    e02 = rho * m02
    e12 = rho * m12
    d22 = rho * rho * m22
    h02 = rho * p0
    x1 = rho * p1
    x2 = rho * rho * p2
    h12 = x1 - h02 * d01
    h22 = x2 - h02 * e02 - h12 * e12
    square = (
        rho * rho * pp + h02 * h02 * n00 + h12 * h12 * d11 + h22 * h22 * d22
        - 2.0 * (h02 * h02 + h12 * x1 + h22 * x2)
        + 2.0 * (h02 * h12 * d01 + h02 * h22 * e02 + h12 * h22 * e12)
    )
    h32 = jnp.sqrt(jnp.maximum(square, 0.0) + EPS)

    c1, s1, r11 = rotation(turned1, h21)
    g1, g2 = c1 * g1, -s1 * g1
    r02 = c0 * h02 + s0 * h12
    turned = c0 * h12 - s0 * h02
    r12 = c1 * turned + s1 * h22
    c2, s2, r22 = rotation(c1 * h22 - s1 * turned, h32)
    g2 = c2 * g2
    y2 = g2 / r22
    y1 = (g1 - r12 * y2) / r11
    y0 = (g0 - (r01 * y1 + r02 * y2)) / r00
    sol_ref[...] = y0 * v0 + y1 * v1 + y2 * v2

    columns = ((h00, h10), (h01, h11, h21), (h02, h12, h22, h32))
    for j, column in enumerate(columns):
        out = jnp.zeros((4, 4), F32)
        for i, value in enumerate(column):
            out = jnp.where(lane[0:4, 0:4] == i, value[0:4, 0:4], out)
        hes_ref[j] = out

    wait_for(send_sem.at[0], ask_out)
    for phase in range(3):
        wait_for(send_sem.at[phase + 1], send.at[phase])
    wait_for(send_sem.at[4], last_in)


def hand_over(answer_ref, hessenberg_ref, answer_out, hessenberg_out):
    answer_out[...] = answer_ref[...]
    hessenberg_out[...] = hessenberg_ref[...]


def solution(mesh):
    def on_device(tile_values, tile_row, tile_slot, tile_count, requests, right_side):
        vmem = pl.BlockSpec(memory_space=pltpu.VMEM)
        smem = pl.BlockSpec(memory_space=pltpu.SMEM)
        hbm = pl.BlockSpec(memory_space=pltpu.HBM)
        shapes = (
            jax.ShapeDtypeStruct((8, 8, 128), F32),
            jax.ShapeDtypeStruct((3, 4, 4), F32),
        )
        answer, hessenberg = pl.pallas_call(
            kernel,
            out_shape=shapes,
            in_specs=[smem, hbm, hbm, hbm, hbm, hbm],
            out_specs=(vmem, vmem),
            scratch_shapes=[
                pltpu.SMEM((TILES,), jnp.int32),
                pltpu.SMEM((TILES,), jnp.int32),
                pltpu.VMEM((1, 128), jnp.int32),
                pltpu.VMEM((8, 8, 128), F32),
                pltpu.VMEM((TILES, 128, 128), F32),
                pltpu.VMEM((PAIRS, 256, 256), BF16),
                pltpu.VMEM((SLOTS, 8, 128), F32),
                pltpu.VMEM((RB, 5, 128), F32),
                pltpu.VMEM((3, N, 5, 128), F32),
                pltpu.VMEM((3, N, 5, 128), F32),
                pltpu.VMEM((N, 1, 128), jnp.int32),
                pltpu.VMEM((N, 1, 128), jnp.int32),
                pltpu.VMEM((1, 128), jnp.int32),
                pltpu.SMEM((1, 128), jnp.int32),
                pltpu.VMEM((1, 128), F32),
                pltpu.VMEM((N, 1, 128), F32),
                pltpu.SemaphoreType.DMA((CHUNKS,)),
                pltpu.SemaphoreType.DMA((4,)),
                pltpu.SemaphoreType.DMA((5,)),
                pltpu.SemaphoreType.DMA((5, 2)),
                pltpu.SemaphoreType.DMA,
            ],
            compiler_params=pltpu.CompilerParams(
                collective_id=0, has_side_effects=True, vmem_limit_bytes=40 << 20
            ),
            name="arnoldi",
        )(
            tile_count,
            *[
                pltpu.with_memory_space_constraint(x, pltpu.HBM)
                for x in (
                    tile_row, tile_slot, tile_values,
                    requests.reshape(1, N), right_side.reshape(8, 8, 128),
                )
            ],
        )
        answer, hessenberg = pl.pallas_call(
            hand_over,
            out_shape=shapes,
            in_specs=[vmem, vmem],
            out_specs=(vmem, vmem),
            compiler_params=pltpu.CompilerParams(vmem_limit_bytes=4 << 20),
            name="hand_over",
        )(answer, hessenberg)
        return answer.reshape(RB, 4, 128), jnp.transpose(hessenberg, (1, 2, 0))

    rows = P("rows")
    return jax.shard_map(
        on_device,
        mesh=mesh,
        in_specs=(rows, rows, rows, rows, rows, rows),
        out_specs=(rows, P()),
        check_vma=False,
    )
```

time: 61.2 us -> 54.6 us (0.89)
  local copies, waits for them, and re-layouts: 4.14 us -> 0 us
  Pallas kernels: 55.5 us -> 53.2 us
    unnamed x2 -> x0, local copies, waits for them, and re-layouts: 2.76 us -> none
    pallas_call x1 -> x2, Pallas kernels: 55.5 us -> 53.2 us  [the longest x1 52.6 us: on_device(): pl.pallas_call(kernel, out_shape=shapes, in_specs=[smem, hbm, hbm, hbm, h...]
    reshape x1 -> x0, local copies, waits for them, and re-layouts: 1.38 us -> none  [on_device(): requests.reshape(N, 1)]
where the time goes in v2:
time: 54.6 us; the launch traced here: 54.5 us
  Pallas kernels  53.2 us (97%)
  between operations  1.29 us (2%)
    pallas_call x1, Pallas kernels, on_device(): pl.pallas_call(kernel, out_shape=shapes, in_specs=[smem, hbm, hbm, hbm, h...  52.6 us

profile of v2, /device:TPU:1, one launch (start us, length us, event | category | flops | bytes accessed | tf_op | source)
XLA Modules:
  0.0 54.5 jit_solution(5224037636291105940)
XLA Ops:
  1.3 52.6 %arnoldi.1 = (f32[8,8,128]{2,1,0:T(8,128)S(1)}, f32[3,4,4]{2,1,0:T(4,128)S(1)}) custom-call(s32[1]{0:T(128)S(6)} %copy.8.count_s, s32[208]{0:T(256)} %row_hbm.1, s32[208]{0:T(256)} %slot_hbm.1, f32[208,128,128]{2,1,0:T(8,128)} %tiles_hbm.1, s32[1,128]{1,0:T(1,128)} %bitcast.5, f32[8,8,128]{2,1,0:T(8,128)} %bitcast.4), custom_call_target="tpu_custom_call" | custom-call | tf_op jit(solution)/shard_map/arnoldi/pallas_call | solution.py:345
  53.9 0.6 %hand_over.1 = (f32[8,8,128]{2,1,0:T(8,128)}, f32[3,4,4]{2,1,0:T(4,128)}) custom-call(f32[8,8,128]{2,1,0:T(8,128)S(1)} %get-tuple-element.6.answer_ref, f32[3,4,4]{2,1,0:T(4,128)S(1)} %get-tuple-element.7.hessenberg_ref), custom_call_target="tpu_custom_call" | custom-call | tf_op jit(solution)/shard_map/hand_over/pallas_call | solution.py:387

commit v3 on v2

--- a/solution.py
+++ b/solution.py
@@ -16,9 +16,7 @@
 PAIRS = TILES // 2
 CHUNK = 16
 CHUNKS = TILES // CHUNK
-AHEAD = 6
-FAR = 4
-ROWS_AHEAD = 32
+ROWS_AHEAD = 12
 
 
 def hops(offset):
@@ -26,9 +24,15 @@
 
 
 OFFSETS = sorted(range(1, N), key=lambda o: (-hops(o), o))
-CHIPS = sorted(range(0, N, 2), key=lambda o: (hops(o), o))
-GROUPS = ([o for o in CHIPS if hops(o) < FAR], [o for o in CHIPS if hops(o) >= FAR])
-COUNTS = (2 * len(GROUPS[0]) - 1, 2 * len(GROUPS[1]))
+BLOCK_ORDER = (6, 5, 4, 3, 2, 1, 0)
+BLOCKS = sorted(range(1, N), key=lambda o: (BLOCK_ORDER.index(hops(o)), o))
+GROUP_HOPS = ((0, 1, 2), (3, 4, 5, 6))
+GROUPS = [[o for o in range(0, N, 2) if hops(o) in group] for group in GROUP_HOPS]
+COUNTS = [sum(hops(o) in group for o in OFFSETS) for group in GROUP_HOPS]
+
+
+def group_of(o):
+    return [i for i, group in enumerate(GROUP_HOPS) if hops(o) in group][0]
 
 
 def partners(me):
@@ -44,7 +48,7 @@
     count_s, row_hbm, slot_hbm, tiles_hbm, req_hbm, b_hbm,
     sol_ref, hes_ref,
     row_s, slot_s, req_ref, b_ref,
-    raw, wide, left, staged, send, got, ask_out, ask_in, ask_row, ask_s, last_out, last_in,
+    raw, wide, left, staged, send, got, ask_in, sums_out, sums_in,
     load_sem, small_sem, send_sem, recv_sem, ask_sem,
 ):
     me = lax.axis_index("rows")
@@ -65,15 +69,15 @@
             ((req_hbm, req_ref), (b_hbm, b_ref), (row_hbm, row_s), (slot_hbm, slot_s))
         )
     ]
-    for copy in small:
+    small[0].start()
+    barrier = pltpu.get_barrier_semaphore()
+    for o in OFFSETS:
+        pl.semaphore_signal(barrier, inc=1, device_id=(partner(o),), device_id_type=MESH)
+    for copy in small[1:]:
         copy.start()
     for c in range(CHUNKS):
         load(c).start()
-    barrier = pltpu.get_barrier_semaphore()
-    for o in OFFSETS:
-        pl.semaphore_signal(barrier, inc=1, device_id=(partner(o),), device_id_type=MESH)
-    for copy in small:
-        copy.wait()
+    small[0].wait()
 
     def split(v):
         hi = v.astype(BF16).astype(F32)
@@ -101,17 +105,15 @@
         whole = like.at[pl.ds(0, count)]
         pltpu.make_async_copy(whole, whole, sem).wait()
 
-    wide_lane = lax.broadcasted_iota(jnp.int32, (N, 128), 1)
-    wanted = jnp.broadcast_to(req_ref[...], (N, 128)).T
-    ask_out[...] = jnp.where(wide_lane == me, wanted, 0).reshape(N, 1, 128)
-
-    lax.fori_loop(0, AHEAD, prepare, 0)
+    own_row = pltpu.make_async_copy(req_ref, ask_in.at[me], ask_sem)
+    own_row.start()
     pl.semaphore_wait(barrier, N - 1)
     for o in OFFSETS:
         to = partner(o)
-        start_send(0, 0, to, ask_out.at[to], ask_in)
-    ask_in[me] = ask_out[me]
-    lax.fori_loop(AHEAD, CHUNKS, prepare, 0)
+        start_send(0, 0, to, req_ref, ask_in)
+    for copy in small[1:]:
+        copy.wait()
+    lax.fori_loop(0, CHUNKS, prepare, 0)
 
     def fold(v):
         return v + pltpu.roll(v, 4, 0)
@@ -135,28 +137,38 @@
             out.append(jnp.broadcast_to(jnp.sum(picked, axis=1, keepdims=True), (8, 128)))
         return out
 
-    def stage(vector, partial):
+    def share(phase, partial):
+        out, into = sums_out.at[phase], sums_in.at[phase]
+        out[...] = partial
+        into[me] = partial
+        for o in OFFSETS:
+            start_send(4 + phase, 0, partner(o), out, into)
+
+    def gathered(phase):
+        into = sums_in.at[phase]
+        wait_for(recv_sem.at[4 + phase, 0], into)
+        return jnp.sum(into[...], axis=0)
+
+    def exchange(phase, vector):
+        out, into = send.at[phase], got.at[phase]
+        blocks = [vector[r // 2][r % 2 * 4 : r % 2 * 4 + 4] for r in range(RB)]
         for r in range(RB):
-            half = (r % 2) * 4
-            block = vector[r // 2][half : half + 4]
-            staged[r] = jnp.concatenate([block, partial], axis=0)
-            hi, lo = split(block)
-            left[r] = jnp.concatenate([hi, lo], axis=0)
-
-    def exchange(phase):
-        out, into = send.at[phase], got.at[phase]
-        targets = [partner(o) for o in OFFSETS] + [me]
+            staged[r] = blocks[r]
+        targets = [partner(o) for o in BLOCKS] + [me]
 
         def fill(i):
-            out[targets[i]] = staged[ask_s[0, targets[i]]]
+            out[targets[i]] = staged[ask_in[targets[i], 0, me]]
 
         for i in range(ROWS_AHEAD):
             fill(i)
-        for i, o in enumerate(OFFSETS):
-            start_send(phase + 1, int(hops(o) >= FAR), targets[i], out.at[targets[i]], into)
+        for i, o in enumerate(BLOCKS):
+            start_send(phase + 1, group_of(o), targets[i], out.at[targets[i]], into)
             if i + ROWS_AHEAD < N:
                 fill(i + ROWS_AHEAD)
-        into[me] = staged[ask_s[0, me]]
+        into[me] = staged[ask_in[me, 0, me]]
+        for r in range(RB):
+            hi, lo = split(blocks[r])
+            left[r] = jnp.concatenate([hi, lo], axis=0)
 
     def times(p, x0, x1):
         x = jnp.concatenate([x0, x1], axis=0).astype(BF16)
@@ -177,7 +189,7 @@
         first = partner(offset) - lax.rem(me, 2)
         x = []
         for d in (first, first + 1):
-            hi, lo = split(into[d][0:4])
+            hi, lo = split(into[d])
             x.append(jnp.concatenate([hi, lo], axis=0))
             left[RB + d] = x[-1]
         y0, y1 = times(RB // 2 + first // 2, x[0], x[1])
@@ -190,31 +202,25 @@
                 acc = add(acc, jnp.where(t < count_s[0], row_s[t], -1), value)
         return acc
 
-    def apply(phase, digest):
-        exchange(phase)
+    def apply(phase, vector, partial, digest):
+        exchange(phase, vector)
+        share(phase, partial())
         into = got.at[phase]
         acc = own_tiles()
-        for group in range(2):
+        for group in range(len(GROUPS)):
             wait_for(recv_sem.at[phase + 1, group], into, COUNTS[group])
-            if group == 1:
-                total = jnp.sum(into[...], axis=0)
-                coefficients = digest(total[4:5])
             for offset in GROUPS[group]:
                 acc = chip_tiles(into, offset, acc)
         acc = extra_tiles(acc)
+        coefficients = digest(gathered(phase))
         acc = [fold(acc[r]) for r in range(RB)]
         z = jnp.stack([jnp.where(low, acc[2 * m], acc[2 * m + 1]) for m in range(RB // 2)])
         return coefficients, z
 
     b = b_ref[...]
-    first_partial = packed([product(b, b)])
-    stage(b, first_partial)
 
     wait_for(recv_sem.at[0, 0], ask_in)
-    ask_row[...] = jnp.sum(ask_in[...], axis=0)
-    to_scalar = pltpu.make_async_copy(ask_row, ask_s, ask_sem)
-    to_scalar.start()
-    to_scalar.wait()
+    own_row.wait()
 
     def digest0(total):
         (bb,) = unpacked(total, 1)
@@ -222,10 +228,9 @@
         inverse = 1.0 / beta
         return beta, inverse, bb * inverse * inverse
 
-    (beta, inverse, n00), z = apply(0, digest0)
+    (beta, inverse, n00), z = apply(0, b, lambda: packed([product(b, b)]), digest0)
     v0 = b * inverse
     t1 = z * inverse
-    stage(t1, packed([product(t1, v0), product(t1, t1)]))
 
     def digest1(total):
         h00, tt = unpacked(total, 2)
@@ -233,13 +238,14 @@
         guess1 = jnp.sqrt(jnp.maximum(square, 0.0) + EPS)
         return h00, guess1, 1.0 / guess1
 
-    (h00, guess1, inverse), z = apply(1, digest1)
+    (h00, guess1, inverse), z = apply(1, t1, lambda: packed([product(t1, v0), product(t1, t1)]), digest1)
     u1 = (t1 - h00 * v0) * inverse
     t2 = (z - h00 * t1) * inverse
-    stage(
-        t2,
-        packed([product(t2, v0), product(t2, u1), product(t2, t2), product(u1, u1), product(u1, v0)]),
-    )
+
+    def partial2():
+        return packed(
+            [product(t2, v0), product(t2, u1), product(t2, t2), product(u1, u1), product(u1, v0)]
+        )
 
     def digest2(total):
         q0, q1, qq, m11, m01 = unpacked(total, 5)
@@ -257,21 +263,21 @@
         guess2 = jnp.sqrt(jnp.maximum(square, 0.0) + EPS)
         return h10, rho, d01, d11, h01, h11, guess2, 1.0 / guess2
 
-    (h10, rho, d01, d11, h01, h11, guess2, inverse), z = apply(2, digest2)
+    (h10, rho, d01, d11, h01, h11, guess2, inverse), z = apply(2, t2, partial2, digest2)
     v1 = u1 * rho
-    t2 = t2 * rho
-    u2 = (t2 - h01 * v0 - h11 * v1) * inverse
-    t3 = (z * rho - h01 * t1 - h11 * t2) * inverse
-
-    last_out[...] = packed(
-        [
-            product(t3, v0), product(t3, v1), product(t3, u2), product(t3, t3),
-            product(u2, u2), product(u2, v0), product(u2, v1),
-        ]
+    s2 = t2 * rho
+    u2 = (s2 - h01 * v0 - h11 * v1) * inverse
+    t3 = (z * rho - h01 * t1 - h11 * s2) * inverse
+
+    share(
+        3,
+        packed(
+            [
+                product(t3, v0), product(t3, v1), product(t3, u2), product(t3, t3),
+                product(u2, u2), product(u2, v0), product(u2, v1),
+            ]
+        ),
     )
-    last_in[me] = last_out[...]
-    for o in OFFSETS:
-        start_send(4, 0, partner(o), last_out, last_in)
 
     def rotation(a, c):
         radius = jnp.sqrt(a * a + c * c)
@@ -282,9 +288,7 @@
     r01 = c0 * h01 + s0 * h11
     turned1 = c0 * h11 - s0 * h01
 
-    wait_for(recv_sem.at[4, 0], last_in)
-    total = jnp.sum(last_in[...], axis=0)
-    p0, p1, p2, pp, m22, m02, m12 = unpacked(total, 7)
+    p0, p1, p2, pp, m22, m02, m12 = unpacked(gathered(3), 7)
     h21 = jnp.sqrt(guess2 * guess2 * m22 + EPS)
     rho = guess2 / h21
     v2 = u2 * rho
@@ -322,10 +326,11 @@
             out = jnp.where(lane[0:4, 0:4] == i, value[0:4, 0:4], out)
         hes_ref[j] = out
 
-    wait_for(send_sem.at[0], ask_out)
+    wait_for(send_sem.at[0], sums_in.at[0])
     for phase in range(3):
         wait_for(send_sem.at[phase + 1], send.at[phase])
-    wait_for(send_sem.at[4], last_in)
+    for phase in range(4):
+        wait_for(send_sem.at[4 + phase], sums_in.at[phase])
 
 
 def hand_over(answer_ref, hessenberg_ref, answer_out, hessenberg_out):
@@ -355,19 +360,16 @@
                 pltpu.VMEM((TILES, 128, 128), F32),
                 pltpu.VMEM((PAIRS, 256, 256), BF16),
                 pltpu.VMEM((SLOTS, 8, 128), F32),
-                pltpu.VMEM((RB, 5, 128), F32),
-                pltpu.VMEM((3, N, 5, 128), F32),
-                pltpu.VMEM((3, N, 5, 128), F32),
-                pltpu.VMEM((N, 1, 128), jnp.int32),
-                pltpu.VMEM((N, 1, 128), jnp.int32),
-                pltpu.VMEM((1, 128), jnp.int32),
-                pltpu.SMEM((1, 128), jnp.int32),
-                pltpu.VMEM((1, 128), F32),
-                pltpu.VMEM((N, 1, 128), F32),
+                pltpu.VMEM((RB, 4, 128), F32),
+                pltpu.VMEM((3, N, 4, 128), F32),
+                pltpu.VMEM((3, N, 4, 128), F32),
+                pltpu.SMEM((N, 1, 128), jnp.int32),
+                pltpu.VMEM((4, 1, 128), F32),
+                pltpu.VMEM((4, N, 1, 128), F32),
                 pltpu.SemaphoreType.DMA((CHUNKS,)),
                 pltpu.SemaphoreType.DMA((4,)),
-                pltpu.SemaphoreType.DMA((5,)),
-                pltpu.SemaphoreType.DMA((5, 2)),
+                pltpu.SemaphoreType.DMA((8,)),
+                pltpu.SemaphoreType.DMA((8, 2)),
                 pltpu.SemaphoreType.DMA,
             ],
             compiler_params=pltpu.CompilerParams(

time: 54.6 us -> 50.6 us (0.927)
  Pallas kernels: 53.2 us -> 49.2 us
    pallas_call x1, Pallas kernels: 52.6 us -> 48.6 us  [on_device(): pl.pallas_call(kernel, out_shape=shapes, in_specs=[smem, hbm, hbm, hbm, h...]
where the time goes in v3:
time: 50.6 us; the launch traced here: 50.5 us
  Pallas kernels  49.2 us (97%)
  between operations  1.29 us (3%)
    pallas_call x1, Pallas kernels, on_device(): pl.pallas_call(kernel, out_shape=shapes, in_specs=[smem, hbm, hbm, hbm, h...  48.6 us

profile of v3, /device:TPU:1, one launch (start us, length us, event | category | flops | bytes accessed | tf_op | source)
XLA Modules:
  0.0 50.5 jit_solution(8093124061558597164)
XLA Ops:
  1.3 48.6 %arnoldi.1 = (f32[8,8,128]{2,1,0:T(8,128)S(1)}, f32[3,4,4]{2,1,0:T(4,128)S(1)}) custom-call(s32[1]{0:T(128)S(6)} %copy.8.count_s, s32[208]{0:T(256)} %row_hbm.1, s32[208]{0:T(256)} %slot_hbm.1, f32[208,128,128]{2,1,0:T(8,128)} %tiles_hbm.1, s32[1,128]{1,0:T(1,128)} %bitcast.5, f32[8,8,128]{2,1,0:T(8,128)} %bitcast.4), custom_call_target="tpu_custom_call" | custom-call | tf_op jit(solution)/shard_map/arnoldi/pallas_call | solution.py:350
  49.9 0.6 %hand_over.1 = (f32[8,8,128]{2,1,0:T(8,128)}, f32[3,4,4]{2,1,0:T(4,128)}) custom-call(f32[8,8,128]{2,1,0:T(8,128)S(1)} %get-tuple-element.6.answer_ref, f32[3,4,4]{2,1,0:T(4,128)S(1)} %get-tuple-element.7.hessenberg_ref), custom_call_target="tpu_custom_call" | custom-call | tf_op jit(solution)/shard_map/hand_over/pallas_call | solution.py:389

commit v4 on v3

--- a/solution.py
+++ b/solution.py
@@ -26,7 +26,7 @@
 OFFSETS = sorted(range(1, N), key=lambda o: (-hops(o), o))
 BLOCK_ORDER = (6, 5, 4, 3, 2, 1, 0)
 BLOCKS = sorted(range(1, N), key=lambda o: (BLOCK_ORDER.index(hops(o)), o))
-GROUP_HOPS = ((0, 1, 2), (3, 4, 5, 6))
+GROUP_HOPS = ((4, 5, 6), (0, 1, 2, 3))
 GROUPS = [[o for o in range(0, N, 2) if hops(o) in group] for group in GROUP_HOPS]
 COUNTS = [sum(hops(o) in group for o in OFFSETS) for group in GROUP_HOPS]
 
@@ -147,7 +147,8 @@
     def gathered(phase):
         into = sums_in.at[phase]
         wait_for(recv_sem.at[4 + phase, 0], into)
-        return jnp.sum(into[...], axis=0)
+        quarters = [jnp.sum(into[pl.ds(i * 32, 32)], axis=0) for i in range(4)]
+        return (quarters[0] + quarters[1]) + (quarters[2] + quarters[3])
 
     def exchange(phase, vector):
         out, into = send.at[phase], got.at[phase]

time: 50.6 us -> 50.4 us (level)
  no operation moved by 1% of the time
where the time goes in v4:
time: 50.4 us; the launch traced here: 50.3 us
  Pallas kernels  49 us (97%)
  between operations  1.29 us (3%)
    pallas_call x1, Pallas kernels, on_device(): pl.pallas_call(kernel, out_shape=shapes, in_specs=[smem, hbm, hbm, hbm, h...  48.4 us

profile of v4, /device:TPU:1, one launch (start us, length us, event | category | flops | bytes accessed | tf_op | source)
XLA Modules:
  0.0 50.3 jit_solution(18109557714561648073)
XLA Ops:
  1.3 48.4 %arnoldi.1 = (f32[8,8,128]{2,1,0:T(8,128)S(1)}, f32[3,4,4]{2,1,0:T(4,128)S(1)}) custom-call(s32[1]{0:T(128)S(6)} %copy.8.count_s, s32[208]{0:T(256)} %row_hbm.1, s32[208]{0:T(256)} %slot_hbm.1, f32[208,128,128]{2,1,0:T(8,128)} %tiles_hbm.1, s32[1,128]{1,0:T(1,128)} %bitcast.5, f32[8,8,128]{2,1,0:T(8,128)} %bitcast.4), custom_call_target="tpu_custom_call" | custom-call | tf_op jit(solution)/shard_map/arnoldi/pallas_call | solution.py:351
  49.6 0.6 %hand_over.1 = (f32[8,8,128]{2,1,0:T(8,128)}, f32[3,4,4]{2,1,0:T(4,128)}) custom-call(f32[8,8,128]{2,1,0:T(8,128)S(1)} %get-tuple-element.6.answer_ref, f32[3,4,4]{2,1,0:T(4,128)S(1)} %get-tuple-element.7.hessenberg_ref), custom_call_target="tpu_custom_call" | custom-call | tf_op jit(solution)/shard_map/hand_over/pallas_call | solution.py:390

commit v5 on v4

--- a/solution.py
+++ b/solution.py
@@ -48,8 +48,8 @@
     count_s, row_hbm, slot_hbm, tiles_hbm, req_hbm, b_hbm,
     sol_ref, hes_ref,
     row_s, slot_s, req_ref, b_ref,
-    raw, wide, left, staged, send, got, ask_in, sums_out, sums_in,
-    load_sem, small_sem, send_sem, recv_sem, ask_sem,
+    raw, wide, left, staged, send, got, ask_in, sums_out, sums_in, mate_out, mate_in,
+    load_sem, small_sem, send_sem, recv_sem, ask_sem, mate_sem,
 ):
     me = lax.axis_index("rows")
     partner = partners(me)
@@ -137,6 +137,36 @@
             out.append(jnp.broadcast_to(jnp.sum(picked, axis=1, keepdims=True), (8, 128)))
         return out
 
+    def share_by_chip(phase, partial):
+        mate = partner(1)
+        own_out, own_in = mate_out.at[phase], mate_in.at[phase]
+        own_out[...] = partial
+        hand = pltpu.make_async_remote_copy(
+            src_ref=own_out, dst_ref=own_in, send_sem=mate_sem.at[phase, 0],
+            recv_sem=mate_sem.at[phase, 1], device_id=(mate,), device_id_type=MESH,
+        )
+        hand.start()
+        acc = own_tiles()
+        hand.wait()
+        both = partial + own_in[...]
+        out, into = sums_out.at[phase], sums_in.at[phase]
+        out[...] = both
+        chip = lax.div(me, 2)
+        into[chip] = both
+        for o in OFFSETS:
+            if o % 2 == 0:
+                pltpu.make_async_remote_copy(
+                    src_ref=out, dst_ref=into.at[chip], send_sem=send_sem.at[4 + phase],
+                    recv_sem=recv_sem.at[4 + phase, 0], device_id=(partner(o),), device_id_type=MESH,
+                ).start()
+        return acc
+
+    def gathered_by_chip(phase):
+        into = sums_in.at[phase]
+        wait_for(recv_sem.at[4 + phase, 0], into, N // 2 - 1)
+        quarters = [jnp.sum(into[pl.ds(i * 16, 16)], axis=0) for i in range(4)]
+        return (quarters[0] + quarters[1]) + (quarters[2] + quarters[3])
+
     def share(phase, partial):
         out, into = sums_out.at[phase], sums_in.at[phase]
         out[...] = partial
@@ -205,15 +235,14 @@
 
     def apply(phase, vector, partial, digest):
         exchange(phase, vector)
-        share(phase, partial())
+        acc = share_by_chip(phase, partial())
         into = got.at[phase]
-        acc = own_tiles()
         for group in range(len(GROUPS)):
             wait_for(recv_sem.at[phase + 1, group], into, COUNTS[group])
             for offset in GROUPS[group]:
                 acc = chip_tiles(into, offset, acc)
         acc = extra_tiles(acc)
-        coefficients = digest(gathered(phase))
+        coefficients = digest(gathered_by_chip(phase))
         acc = [fold(acc[r]) for r in range(RB)]
         z = jnp.stack([jnp.where(low, acc[2 * m], acc[2 * m + 1]) for m in range(RB // 2)])
         return coefficients, z
@@ -331,7 +360,7 @@
     for phase in range(3):
         wait_for(send_sem.at[phase + 1], send.at[phase])
     for phase in range(4):
-        wait_for(send_sem.at[4 + phase], sums_in.at[phase])
+        wait_for(send_sem.at[4 + phase], sums_in.at[phase], N - 1 if phase == 3 else N // 2 - 1)
 
 
 def hand_over(answer_ref, hessenberg_ref, answer_out, hessenberg_out):
@@ -367,11 +396,14 @@
                 pltpu.SMEM((N, 1, 128), jnp.int32),
                 pltpu.VMEM((4, 1, 128), F32),
                 pltpu.VMEM((4, N, 1, 128), F32),
+                pltpu.VMEM((3, 1, 128), F32),
+                pltpu.VMEM((3, 1, 128), F32),
                 pltpu.SemaphoreType.DMA((CHUNKS,)),
                 pltpu.SemaphoreType.DMA((4,)),
                 pltpu.SemaphoreType.DMA((8,)),
                 pltpu.SemaphoreType.DMA((8, 2)),
                 pltpu.SemaphoreType.DMA,
+                pltpu.SemaphoreType.DMA((3, 2)),
             ],
             compiler_params=pltpu.CompilerParams(
                 collective_id=0, has_side_effects=True, vmem_limit_bytes=40 << 20

time: 50.4 us -> 50.1 us (level)
  no operation moved by 1% of the time
where the time goes in v5:
time: 50.1 us; the launch traced here: 50 us
  Pallas kernels  48.7 us (97%)
  between operations  1.29 us (3%)
    pallas_call x1, Pallas kernels, on_device(): pl.pallas_call(kernel, out_shape=shapes, in_specs=[smem, hbm, hbm, hbm, h...  48.1 us

profile of v5, /device:TPU:1, one launch (start us, length us, event | category | flops | bytes accessed | tf_op | source)
XLA Modules:
  0.0 50.0 jit_solution(5898461665684986299)
XLA Ops:
  1.3 48.1 %arnoldi.1 = (f32[8,8,128]{2,1,0:T(8,128)S(1)}, f32[3,4,4]{2,1,0:T(4,128)S(1)}) custom-call(s32[1]{0:T(128)S(6)} %copy.8.count_s, s32[208]{0:T(256)} %row_hbm.1, s32[208]{0:T(256)} %slot_hbm.1, f32[208,128,128]{2,1,0:T(8,128)} %tiles_hbm.1, s32[1,128]{1,0:T(1,128)} %bitcast.5, f32[8,8,128]{2,1,0:T(8,128)} %bitcast.4), custom_call_target="tpu_custom_call" | custom-call | tf_op jit(solution)/shard_map/arnoldi/pallas_call | solution.py:380
  49.4 0.6 %hand_over.1 = (f32[8,8,128]{2,1,0:T(8,128)}, f32[3,4,4]{2,1,0:T(4,128)}) custom-call(f32[8,8,128]{2,1,0:T(8,128)S(1)} %get-tuple-element.6.answer_ref, f32[3,4,4]{2,1,0:T(4,128)S(1)} %get-tuple-element.7.hessenberg_ref), custom_call_target="tpu_custom_call" | custom-call | tf_op jit(solution)/shard_map/hand_over/pallas_call | solution.py:422
